TPU v7x, 256 devices: a whole 4x4x8 slice. The times are simulated.
256 devices in a mesh: rows: 32 (over x, y, core), grp: 8 (over z).
Axes of the slice: x: 4, y: 4, z: 8, core: 2. Of those that a mesh axis runs over, the one named last changes fastest.
Arguments:
- factor: float32 [65536, 1024], P(('rows', 'grp')), as said below
- start_block: float32 [1024, 256], replicated, may hold values from -6 to 6
Outputs:
- compressed: float32 [65536, 256], P(('rows', 'grp'))
- tail_share: float32 [], replicated
Inputs may be any that keep to these rules, and one draw needn't show every extreme that they name: Every entry is finite; the factor has full column rank.
All inputs are finite; a program needn't handle non-finite values.
Results may differ from a plain program's by a relative error of at most 0.0007.
Values sent between devices are 32-bit elements; how exact they have to be, the bound alone decides.
A program may use at most 64 MiB of HBM per device.

v0:
```python
import functools
import math

import jax
import jax.numpy as jnp
from jax import lax
from jax.experimental import pallas as pl
from jax.experimental.pallas import tpu as pltpu
from jax.sharding import PartitionSpec as P

AXES = ("rows", "grp")
HI = lax.Precision.HIGHEST
B = 16
F32 = jnp.float32


def contract(a, b, da, db):
    return lax.dot_general(a, b, (((da,), (db,)), ((), ())), precision=HI, preferred_element_type=F32)


def split3(x):
    a = x.astype(jnp.bfloat16).astype(F32)
    rest = x - a
    b = rest.astype(jnp.bfloat16).astype(F32)
    return a, b, (rest - b).astype(jnp.bfloat16).astype(F32)


def factor_step(m_ref, k):
    n = m_ref.shape[1]
    per = 128 // B
    row0 = pl.multiple_of(k * B, B)
    half = pl.multiple_of((k // per) * 128, 128)
    lane0 = (k % per) * B
    rows8 = lax.broadcasted_iota(jnp.int32, (8, 128), 0)
    diag = [m_ref[pl.ds(row0 + 8 * g, 8), pl.ds(half, 128)] for g in range(2)]
    column = {}
    for c in range(B):
        idx = jnp.full((8, 128), lane0 + c, jnp.int32)
        for g in range(2):
            if 8 * g + 8 > c:
                column[c, g] = jnp.take_along_axis(diag[g], idx, axis=1)
    lanes = lax.broadcasted_iota(jnp.int32, (8, n), 1) - k * B
    in_block = (lanes >= 0) & (lanes < B)
    wide = []
    for g in range(2):
        unit = jnp.where(lanes == 8 * g + lax.broadcasted_iota(jnp.int32, (8, n), 0), 1.0, 0.0)
        wide.append(jnp.where(in_block, unit, m_ref[pl.ds(row0 + 8 * g, 8), :]))
    pivots = [jnp.ones((8, 128), F32) for _ in range(2)]
    for c in range(B):
        gc, rc = divmod(c, 8)
        pivot = jnp.broadcast_to(column[c, gc][rc : rc + 1, :], (8, 128))
        pivots[gc] = jnp.where(rows8 == rc, pivot, pivots[gc])
        scale = 1.0 / pivot
        mult = {g: column[c, g] * scale for g in range(gc, 2)}
        mult[gc] = jnp.where(rows8 > rc, mult[gc], 0.0)
        pivot_row = jnp.broadcast_to(wide[gc][rc : rc + 1, :], (8, n))
        for d in range(c + 1, B):
            gd, rd = divmod(d, 8)
            entry = jnp.broadcast_to(column[c, gd][rd : rd + 1, :], (8, 128))
            for g in range(gd, 2):
                column[d, g] = column[d, g] - mult[g] * entry
        for g in range(gc, 2):
            wide[g] = wide[g] - jnp.tile(mult[g], (1, n // 128)) * pivot_row
    final = []
    for g in range(2):
        s = lax.rsqrt(pivots[g])
        s = s * (1.5 - 0.5 * pivots[g] * s * s)
        final.append(wide[g] * jnp.tile(s, (1, n // 128)))
    u = jnp.concatenate(final, axis=0)
    a, b, c = split3(u)
    right = jnp.concatenate([a, b, a, c, b, a], axis=0).astype(jnp.bfloat16)
    later = lax.broadcasted_iota(jnp.int32, (B, n), 1) >= (k + 1) * B
    a, b, c = (jnp.where(later, t, 0.0) for t in (a, b, c))
    left = jnp.concatenate([a, a, b, a, b, c], axis=0).T.astype(jnp.bfloat16)
    update = jnp.dot(left, right, preferred_element_type=F32)
    cols = lax.broadcasted_iota(jnp.int32, (n, n), 1) - k * B
    m_ref[...] = jnp.where((cols >= 0) & (cols < B), 0.0, m_ref[...]) - update
    m_ref[pl.ds(row0, B), :] = u


def factor_steps(m_ref, lo, hi):
    def body(k, carry):
        factor_step(m_ref, k)
        return carry

    lax.fori_loop(lo, hi, body, 0)


def kernel(
    sizes,
    z_ref,
    s_ref,
    c_ref,
    tail_ref,
    w_ref,
    x_ref,
    pair_ref,
    plane_ref,
    slab_ref,
    line_ref,
    full_ref,
    m1_ref,
    m2_ref,
    e_ref,
    ep_ref,
    eq_ref,
    *sems,
):
    nx, ny, nz = sizes
    (pair_s, pair_r, plane_s, plane_r, line_s, line_r, zg_s, zg_r, pg_s, pg_r, fw_s, fw_r, ep_s, ep_r, eq_s, eq_r) = sems
    nq = nx * ny
    rank, depth = s_ref.shape[1], s_ref.shape[0]
    half = rank // 2
    rows, cols = half // nq, depth // nz
    me = lax.axis_index("rows")
    mz = lax.axis_index("grp")
    mc = me % 2
    mq = me // 2
    mx, my = mq // ny, mq % ny

    def at(q, c, z):
        return {"rows": q * 2 + c, "grp": z}

    def plane_peer(dx, dy):
        return ((mx + dx) % nx) * ny + (my + dy) % ny

    far = lambda d, n: min(d, n - d)
    plane = [(dx, dy) for dx in range(nx) for dy in range(ny) if dx or dy]
    plane.sort(key=lambda d: (-far(d[0], nx) - far(d[1], ny), d))
    line = sorted(range(1, nz), key=lambda d: (-far(d, nz), d))
    other = 1 - mc

    barrier = pltpu.get_barrier_semaphore()
    greet = [at(mq, other, mz)]
    greet += [at(plane_peer(dx, dy), mc, mz) for dx, dy in plane]
    greet += [at(mq, mc, (mz + dz) % nz) for dz in line]
    greet += [at(mq, other, (mz + dz) % nz) for dz in line]
    for device in greet:
        pl.semaphore_signal(barrier, inc=1, device_id=device, device_id_type=pl.DeviceIdType.MESH)

    def remote(src, dst, send, recv, device):
        return pltpu.make_async_remote_copy(
            src_ref=src, dst_ref=dst, send_sem=send, recv_sem=recv, device_id=device, device_id_type=pl.DeviceIdType.MESH
        )

    def half_rows(c):
        return pl.ds(pl.multiple_of(c * half, half), half)

    def slab_rows(c, q):
        return pl.ds(pl.multiple_of(c * half + q * rows, rows), rows)

    def slab_cols(z):
        return pl.ds(pl.multiple_of(z * cols, cols), cols)

    w_ref[...] = contract(z_ref[...], s_ref[...], 1, 0)
    x_ref[half_rows(other), :] = contract(w_ref[:, half_rows(other)], z_ref[...], 0, 0)
    pl.semaphore_wait(barrier, len(greet))
    pair = remote(x_ref.at[half_rows(other), :], pair_ref, pair_s, pair_r, at(mq, other, mz))
    pair.start()
    x_ref[half_rows(mc), :] = contract(w_ref[:, half_rows(mc)], z_ref[...], 0, 0)
    pair.wait()
    x_ref[half_rows(mc), :] = x_ref[half_rows(mc), :] + pair_ref[...]

    copies = []
    for j, (dx, dy) in enumerate(plane):
        q = plane_peer(dx, dy)
        copies.append(remote(x_ref.at[slab_rows(mc, q), :], plane_ref.at[j], plane_s.at[j], plane_r.at[j], at(q, mc, mz)))
        copies[-1].start()
    m1_ref[...] = contract(s_ref[...], s_ref[...], 0, 0)
    steps = rank // B
    cut1, cut2, cut3 = steps * 7 // 16, steps * 11 // 16, steps
    factor_steps(m1_ref, 0, cut1)
    total = x_ref[slab_rows(mc, mq), :]
    for j, copy in enumerate(copies):
        copy.wait_recv()
        total = total + plane_ref[j]
    slab_ref[...] = total
    lines = []
    for j, dz in enumerate(line):
        z = (mz + dz) % nz
        lines.append(remote(slab_ref.at[:, slab_cols(z)], line_ref.at[j], line_s.at[j], line_r.at[j], at(mq, mc, z)))
        lines[-1].start()
    factor_steps(m1_ref, cut1, cut2)
    total = slab_ref[:, slab_cols(mz)]
    for j, copy in enumerate(lines):
        copy.wait_recv()
        total = total + line_ref[j]
    full_ref[slab_rows(mc, mq), slab_cols(mz)] = total

    tile = full_ref.at[slab_rows(mc, mq), slab_cols(mz)]
    tiles = []
    for j, dz in enumerate(line):
        tiles.append(remote(tile, tile, zg_s.at[j], zg_r.at[j], at(mq, mc, (mz + dz) % nz)))
        tiles[-1].start()
    factor_steps(m1_ref, cut2, cut3)
    for copy in tiles:
        copy.wait_recv()
    slab = full_ref.at[slab_rows(mc, mq), :]
    slabs = []
    for j, (dx, dy) in enumerate(plane):
        slabs.append(remote(slab, slab, pg_s.at[j], pg_r.at[j], at(plane_peer(dx, dy), mc, mz)))
        slabs[-1].start()
    forwards = [remote(slab, slab, fw_s.at[nq - 1], fw_r.at[nq - 1], at(mq, other, mz))]
    forwards[0].start()
    energy_all = jnp.sum(z_ref[...] * z_ref[...])
    for j in reversed(range(len(plane))):
        dx, dy = plane[j]
        slabs[j].wait_recv()
        block = full_ref.at[slab_rows(mc, plane_peer(-dx, -dy)), :]
        forwards.append(remote(block, block, fw_s.at[j], fw_r.at[j], at(mq, other, mz)))
        forwards[-1].start()
    for copy in forwards:
        copy.wait_recv()
    for copy in copies:
        copy.wait_send()

    x_ref[...] = contract(m1_ref[...], full_ref[...], 1, 0)
    m2_ref[...] = contract(x_ref[...], x_ref[...], 1, 1)
    w_ref[...] = contract(z_ref[...], x_ref[...], 1, 1)
    factor_steps(m2_ref, 0, steps)
    compressed = contract(w_ref[...], m2_ref[...], 1, 1)
    c_ref[...] = compressed
    energy_kept = jnp.sum(compressed * compressed)

    lane = lax.broadcasted_iota(jnp.int32, (1, 128), 1)
    e_ref[...] = jnp.where(lane == 0, energy_kept, jnp.where(lane == 1, energy_all, 0.0))
    ep_ref[mq] = e_ref[...]
    first = []
    for j, (dx, dy) in enumerate(plane):
        first.append(remote(e_ref, ep_ref.at[mq], ep_s.at[j], ep_r.at[j], at(plane_peer(dx, dy), mc, mz)))
        first[-1].start()
    for copy in first:
        copy.wait()
    e_ref[...] = functools.reduce(jnp.add, [ep_ref[q] for q in range(nq)])
    spot = mz * 2 + mc
    eq_ref[spot] = e_ref[...]
    second = []
    for j, (dz, dc) in enumerate([(dz, dc) for dc in range(2) for dz in [*line, 0] if dz or dc]):
        second.append(
            remote(e_ref, eq_ref.at[spot], eq_s.at[j], eq_r.at[j], at(mq, (mc + dc) % 2, (mz + dz) % nz))
        )
        second[-1].start()
    for copy in second:
        copy.wait()
    sums = functools.reduce(jnp.add, [eq_ref[i] for i in range(2 * nz)])
    tail_ref[...] = 1.0 - sums[:, 0:1] / sums[:, 1:2]
    for copy in [*lines, *tiles, *slabs, *forwards]:
        copy.wait_send()


def local(sizes, factor, start_block):
    nx, ny, nz = sizes
    nq = nx * ny
    depth, rank = start_block.shape
    half = rank // 2
    rows, cols = half // nq, depth // nz
    vmem = pl.BlockSpec(memory_space=pltpu.VMEM)
    dma = pltpu.SemaphoreType.DMA
    compressed, tail = pl.pallas_call(
        functools.partial(kernel, sizes),
        out_shape=(
            jax.ShapeDtypeStruct((factor.shape[0], rank), F32),
            jax.ShapeDtypeStruct((1, 1), F32),
        ),
        in_specs=[vmem, vmem],
        out_specs=(vmem, vmem),
        scratch_shapes=[
            pltpu.VMEM((factor.shape[0], rank), F32),
            pltpu.VMEM((rank, depth), F32),
            pltpu.VMEM((half, depth), F32),
            pltpu.VMEM((nq - 1, rows, depth), F32),
            pltpu.VMEM((rows, depth), F32),
            pltpu.VMEM((nz - 1, rows, cols), F32),
            pltpu.VMEM((rank, depth), F32),
            pltpu.VMEM((rank, rank), F32),
            pltpu.VMEM((rank, rank), F32),
            pltpu.VMEM((1, 128), F32),
            pltpu.VMEM((nq, 1, 128), F32),
            pltpu.VMEM((2 * nz, 1, 128), F32),
            dma,
            dma,
            dma((nq - 1,)),
            dma((nq - 1,)),
            dma((nz - 1,)),
            dma((nz - 1,)),
            dma((nz - 1,)),
            dma((nz - 1,)),
            dma((nq - 1,)),
            dma((nq - 1,)),
            dma((nq,)),
            dma((nq,)),
            dma((nq - 1,)),
            dma((nq - 1,)),
            dma((2 * nz - 1,)),
            dma((2 * nz - 1,)),
        ],
        compiler_params=pltpu.CompilerParams(
            collective_id=0, has_side_effects=True, vmem_limit_bytes=40 * 2**20
        ),
    )(factor, start_block)
    return compressed, tail[0, 0]


def solution(mesh):
    side = math.isqrt(mesh.shape["rows"] // 2)
    sizes = (side, side, mesh.shape["grp"])
    return jax.shard_map(
        functools.partial(local, sizes),
        mesh=mesh,
        in_specs=(P(AXES, None), P()),
        out_specs=(P(AXES, None), P()),
        check_vma=False,
    )
```

profile of v0, /device:TPU:1, one launch (start us, length us, event | category | flops | bytes accessed | tf_op | source)
XLA Modules:
  0.0 64.8 jit_solution(15824048445450234708)
XLA Ops:
  0.6 0.0 copy-start
  0.6 1.2 %copy-done = f32[256,1024]{1,0:T(8,128)S(1)} copy-done((f32[256,1024]{1,0:T(8,128)S(1)}, f32[256,1024]{1,0:T(8,128)}, u32[]{:S(2)}) %copy-start) | copy-done | bytes 1048600
  1.9 0.0 copy-start.1
  1.9 1.2 %copy-done.1 = f32[1024,256]{1,0:T(8,128)S(1)} copy-done((f32[1024,256]{1,0:T(8,128)S(1)}, f32[1024,256]{1,0:T(8,128)}, u32[]{:S(2)}) %copy-start.1) | copy-done | bytes 1048600
  3.1 59.3 %shard_map.41 = (f32[256,256]{1,0:T(8,128)S(1)}, f32[1,1]{1,0:T(1,128)}) custom-call(f32[256,1024]{1,0:T(8,128)S(1)} %copy-done, f32[1024,256]{1,0:T(8,128)S(1)} %copy-done.1), custom_call_target="tpu_custom_call" | custom-call | tf_op jit(solution)/shard_map/pallas_call | solution.py:259
  62.4 0.7 %copy.6 = f32[256,256]{1,0:T(8,128)} copy(f32[256,256]{1,0:T(8,128)S(1)} %get-tuple-element.8) | data formatting | bytes 524288
Async XLA Ops:
  0.6 1.2 %copy-start = (f32[256,1024]{1,0:T(8,128)S(1)}, f32[256,1024]{1,0:T(8,128)}, u32[]{:S(2)}) copy-start(f32[256,1024]{1,0:T(8,128)} %z_ref.1) | copy-start | bytes 3145732
  1.9 1.2 %copy-start.1 = (f32[1024,256]{1,0:T(8,128)S(1)}, f32[1024,256]{1,0:T(8,128)}, u32[]{:S(2)}) copy-start(f32[1024,256]{1,0:T(8,128)} %s_ref.1) | copy-start | bytes 3145732
where the time goes:
time: 65 us; the launch traced here: 64.8 us
  Pallas kernels  59.3 us (91%)
  local copies, waits for them, and re-layouts  3.15 us (5%)
  between operations  2.41 us (4%)
    pallas_call x1, Pallas kernels, local(): pl.pallas_call(functools.partial(kernel, sizes), out_shape=(jax.ShapeDtyp...  59.3 us
    unnamed x5, local copies, waits for them, and re-layouts  3.15 us

commit v1 on v0

--- a/solution.py
+++ b/solution.py
@@ -12,6 +12,8 @@
 HI = lax.Precision.HIGHEST
 B = 16
 F32 = jnp.float32
+PARTS = 4
+CUT1, CUT2 = 9, 12
 
 
 def contract(a, b, da, db):
@@ -88,17 +90,19 @@
 
 def kernel(
     sizes,
+    z_hbm,
+    s_hbm,
+    c_ref,
+    tail_ref,
     z_ref,
     s_ref,
-    c_ref,
-    tail_ref,
     w_ref,
     x_ref,
     pair_ref,
     plane_ref,
-    slab_ref,
     line_ref,
     full_ref,
+    part_ref,
     m1_ref,
     m2_ref,
     e_ref,
@@ -107,11 +111,11 @@
     *sems,
 ):
     nx, ny, nz = sizes
-    (pair_s, pair_r, plane_s, plane_r, line_s, line_r, zg_s, zg_r, pg_s, pg_r, fw_s, fw_r, ep_s, ep_r, eq_s, eq_r) = sems
+    (z_in, s_in, pair_s, pair_r, plane_s, plane_r, line_s, line_r, back_s, back_r, fw_s, fw_r, ep_s, ep_r, eq_s, eq_r) = sems
     nq = nx * ny
     rank, depth = s_ref.shape[1], s_ref.shape[0]
     half = rank // 2
-    rows, cols = half // nq, depth // nz
+    rows, cols = half // nq, depth // PARTS
     me = lax.axis_index("rows")
     mz = lax.axis_index("grp")
     mc = me % 2
@@ -129,6 +133,16 @@
     plane.sort(key=lambda d: (-far(d[0], nx) - far(d[1], ny), d))
     line = sorted(range(1, nz), key=lambda d: (-far(d, nz), d))
     other = 1 - mc
+
+    def part(i):
+        return pl.ds(i * cols, cols)
+
+    loads = []
+    for i in range(PARTS):
+        loads.append(pltpu.make_async_copy(z_hbm.at[:, part(i)], z_ref.at[:, part(i)], z_in.at[i]))
+        loads.append(pltpu.make_async_copy(s_hbm.at[part(i), :], s_ref.at[part(i), :], s_in.at[i]))
+    for copy in loads:
+        copy.start()
 
     barrier = pltpu.get_barrier_semaphore()
     greet = [at(mq, other, mz)]
@@ -149,10 +163,11 @@
     def slab_rows(c, q):
         return pl.ds(pl.multiple_of(c * half + q * rows, rows), rows)
 
-    def slab_cols(z):
-        return pl.ds(pl.multiple_of(z * cols, cols), cols)
-
-    w_ref[...] = contract(z_ref[...], s_ref[...], 1, 0)
+    for i in range(PARTS):
+        loads[2 * i].wait()
+        loads[2 * i + 1].wait()
+        term = contract(z_ref[:, part(i)], s_ref[part(i), :], 1, 0)
+        w_ref[...] = term if i == 0 else w_ref[...] + term
     x_ref[half_rows(other), :] = contract(w_ref[:, half_rows(other)], z_ref[...], 0, 0)
     pl.semaphore_wait(barrier, len(greet))
     pair = remote(x_ref.at[half_rows(other), :], pair_ref, pair_s, pair_r, at(mq, other, mz))
@@ -161,62 +176,59 @@
     pair.wait()
     x_ref[half_rows(mc), :] = x_ref[half_rows(mc), :] + pair_ref[...]
 
-    copies = []
-    for j, (dx, dy) in enumerate(plane):
-        q = plane_peer(dx, dy)
-        copies.append(remote(x_ref.at[slab_rows(mc, q), :], plane_ref.at[j], plane_s.at[j], plane_r.at[j], at(q, mc, mz)))
-        copies[-1].start()
+    for i in range(PARTS):
+        for j, (dx, dy) in enumerate(plane):
+            q = plane_peer(dx, dy)
+            remote(
+                x_ref.at[slab_rows(mc, q), part(i)], plane_ref.at[i, j], plane_s.at[i], plane_r.at[i], at(q, mc, mz)
+            ).start()
+
+    def plane_all(i, send, recv):
+        return remote(plane_ref.at[i], plane_ref.at[i], send.at[i], recv.at[i], at(mq, other, mz))
+
+    def line_all(i):
+        most = line_ref.at[i, pl.ds(0, nz - 1)]
+        return remote(most, most, line_s.at[i], line_r.at[i], at(mq, other, mz))
+
     m1_ref[...] = contract(s_ref[...], s_ref[...], 0, 0)
     steps = rank // B
-    cut1, cut2, cut3 = steps * 7 // 16, steps * 11 // 16, steps
+    cut1, cut2 = steps * CUT1 // 16, steps * CUT2 // 16
     factor_steps(m1_ref, 0, cut1)
-    total = x_ref[slab_rows(mc, mq), :]
-    for j, copy in enumerate(copies):
-        copy.wait_recv()
-        total = total + plane_ref[j]
-    slab_ref[...] = total
-    lines = []
-    for j, dz in enumerate(line):
-        z = (mz + dz) % nz
-        lines.append(remote(slab_ref.at[:, slab_cols(z)], line_ref.at[j], line_s.at[j], line_r.at[j], at(mq, mc, z)))
-        lines[-1].start()
+    for i in range(PARTS):
+        plane_all(i, plane_s, plane_r).wait_recv()
+        total = x_ref[slab_rows(mc, mq), part(i)]
+        for j in range(len(plane)):
+            total = total + plane_ref[i, j]
+        line_ref[i, mz] = total
+        own = line_ref.at[i, mz]
+        for dz in line:
+            remote(own, own, line_s.at[i], line_r.at[i], at(mq, mc, (mz + dz) % nz)).start()
     factor_steps(m1_ref, cut1, cut2)
-    total = slab_ref[:, slab_cols(mz)]
-    for j, copy in enumerate(lines):
-        copy.wait_recv()
-        total = total + line_ref[j]
-    full_ref[slab_rows(mc, mq), slab_cols(mz)] = total
-
-    tile = full_ref.at[slab_rows(mc, mq), slab_cols(mz)]
-    tiles = []
-    for j, dz in enumerate(line):
-        tiles.append(remote(tile, tile, zg_s.at[j], zg_r.at[j], at(mq, mc, (mz + dz) % nz)))
-        tiles[-1].start()
-    factor_steps(m1_ref, cut2, cut3)
-    for copy in tiles:
-        copy.wait_recv()
-    slab = full_ref.at[slab_rows(mc, mq), :]
-    slabs = []
-    for j, (dx, dy) in enumerate(plane):
-        slabs.append(remote(slab, slab, pg_s.at[j], pg_r.at[j], at(plane_peer(dx, dy), mc, mz)))
-        slabs[-1].start()
-    forwards = [remote(slab, slab, fw_s.at[nq - 1], fw_r.at[nq - 1], at(mq, other, mz))]
-    forwards[0].start()
+    for i in range(PARTS):
+        line_all(i).wait_recv()
+        full_ref[slab_rows(mc, mq), part(i)] = functools.reduce(jnp.add, [line_ref[i, z] for z in range(nz)])
+        slab = full_ref.at[slab_rows(mc, mq), part(i)]
+        for dx, dy in plane:
+            remote(slab, slab, back_s.at[i], back_r.at[i], at(plane_peer(dx, dy), mc, mz)).start()
+    factor_steps(m1_ref, cut2, steps)
     energy_all = jnp.sum(z_ref[...] * z_ref[...])
-    for j in reversed(range(len(plane))):
-        dx, dy = plane[j]
-        slabs[j].wait_recv()
-        block = full_ref.at[slab_rows(mc, plane_peer(-dx, -dy)), :]
-        forwards.append(remote(block, block, fw_s.at[j], fw_r.at[j], at(mq, other, mz)))
-        forwards[-1].start()
-    for copy in forwards:
-        copy.wait_recv()
-    for copy in copies:
-        copy.wait_send()
-
-    x_ref[...] = contract(m1_ref[...], full_ref[...], 1, 0)
-    m2_ref[...] = contract(x_ref[...], x_ref[...], 1, 1)
-    w_ref[...] = contract(z_ref[...], x_ref[...], 1, 1)
+
+    def forward(i):
+        block = full_ref.at[half_rows(mc), part(i)]
+        return remote(block, block, fw_s.at[i], fw_r.at[i], at(mq, other, mz))
+
+    for i in range(PARTS + 1):
+        if i < PARTS:
+            plane_all(i, back_s, back_r).wait_recv()
+            forward(i).start()
+        if i > 0:
+            forward(i - 1).wait_recv()
+            part_ref[...] = contract(m1_ref[...], full_ref[:, part(i - 1)], 1, 0)
+            square = contract(part_ref[...], part_ref[...], 1, 1)
+            m2_ref[...] = square if i == 1 else m2_ref[...] + square
+            term = contract(z_ref[:, part(i - 1)], part_ref[...], 1, 1)
+            w_ref[...] = term if i == 1 else w_ref[...] + term
+
     factor_steps(m2_ref, 0, steps)
     compressed = contract(w_ref[...], m2_ref[...], 1, 1)
     c_ref[...] = compressed
@@ -240,12 +252,15 @@
             remote(e_ref, eq_ref.at[spot], eq_s.at[j], eq_r.at[j], at(mq, (mc + dc) % 2, (mz + dz) % nz))
         )
         second[-1].start()
+    for i in range(PARTS):
+        plane_all(i, plane_s, plane_r).wait_send()
+        line_all(i).wait_send()
+        plane_all(i, back_s, back_r).wait_send()
+        forward(i).wait_send()
     for copy in second:
         copy.wait()
     sums = functools.reduce(jnp.add, [eq_ref[i] for i in range(2 * nz)])
     tail_ref[...] = 1.0 - sums[:, 0:1] / sums[:, 1:2]
-    for copy in [*lines, *tiles, *slabs, *forwards]:
-        copy.wait_send()
 
 
 def local(sizes, factor, start_block):
@@ -253,8 +268,9 @@
     nq = nx * ny
     depth, rank = start_block.shape
     half = rank // 2
-    rows, cols = half // nq, depth // nz
+    rows, cols = half // nq, depth // PARTS
     vmem = pl.BlockSpec(memory_space=pltpu.VMEM)
+    hbm = pl.BlockSpec(memory_space=pltpu.HBM)
     dma = pltpu.SemaphoreType.DMA
     compressed, tail = pl.pallas_call(
         functools.partial(kernel, sizes),
@@ -262,33 +278,28 @@
             jax.ShapeDtypeStruct((factor.shape[0], rank), F32),
             jax.ShapeDtypeStruct((1, 1), F32),
         ),
-        in_specs=[vmem, vmem],
+        in_specs=[hbm, hbm],
         out_specs=(vmem, vmem),
         scratch_shapes=[
+            pltpu.VMEM(factor.shape, F32),
+            pltpu.VMEM(start_block.shape, F32),
             pltpu.VMEM((factor.shape[0], rank), F32),
             pltpu.VMEM((rank, depth), F32),
             pltpu.VMEM((half, depth), F32),
-            pltpu.VMEM((nq - 1, rows, depth), F32),
-            pltpu.VMEM((rows, depth), F32),
-            pltpu.VMEM((nz - 1, rows, cols), F32),
+            pltpu.VMEM((PARTS, nq - 1, rows, cols), F32),
+            pltpu.VMEM((PARTS, nz, rows, cols), F32),
             pltpu.VMEM((rank, depth), F32),
+            pltpu.VMEM((rank, cols), F32),
             pltpu.VMEM((rank, rank), F32),
             pltpu.VMEM((rank, rank), F32),
             pltpu.VMEM((1, 128), F32),
             pltpu.VMEM((nq, 1, 128), F32),
             pltpu.VMEM((2 * nz, 1, 128), F32),
+            dma((PARTS,)),
+            dma((PARTS,)),
             dma,
             dma,
-            dma((nq - 1,)),
-            dma((nq - 1,)),
-            dma((nz - 1,)),
-            dma((nz - 1,)),
-            dma((nz - 1,)),
-            dma((nz - 1,)),
-            dma((nq - 1,)),
-            dma((nq - 1,)),
-            dma((nq,)),
-            dma((nq,)),
+            *[dma((PARTS,)) for _ in range(8)],
             dma((nq - 1,)),
             dma((nq - 1,)),
             dma((2 * nz - 1,)),

time: 65 us -> 60.4 us (0.929)
  Pallas kernels: 59.3 us -> 54.6 us
    pallas_call x1, Pallas kernels: 59.3 us -> 54.6 us  [local(): pl.pallas_call(functools.partial(kernel, sizes), out_shape=(jax.ShapeDtyp...]
where the time goes in v1:
time: 60.4 us; the launch traced here: 60.2 us
  Pallas kernels  54.6 us (90%)
  local copies, waits for them, and re-layouts  3.15 us (5%)
  between operations  2.41 us (4%)
    pallas_call x1, Pallas kernels, local(): pl.pallas_call(functools.partial(kernel, sizes), out_shape=(jax.ShapeDtyp...  54.6 us
    unnamed x5, local copies, waits for them, and re-layouts  3.15 us

profile of v1, /device:TPU:1, one launch (start us, length us, event | category | flops | bytes accessed | tf_op | source)
XLA Modules:
  0.0 60.2 jit_solution(14259191808293300525)
XLA Ops:
  0.6 0.0 copy-start
  0.6 1.2 %copy-done = f32[256,1024]{1,0:T(8,128)S(1)} copy-done((f32[256,1024]{1,0:T(8,128)S(1)}, f32[256,1024]{1,0:T(8,128)}, u32[]{:S(2)}) %copy-start) | copy-done | bytes 1048600
  1.9 0.0 copy-start.1
  1.9 1.2 %copy-done.1 = f32[1024,256]{1,0:T(8,128)S(1)} copy-done((f32[1024,256]{1,0:T(8,128)S(1)}, f32[1024,256]{1,0:T(8,128)}, u32[]{:S(2)}) %copy-start.1) | copy-done | bytes 1048600
  3.1 54.6 %shard_map.41 = (f32[256,256]{1,0:T(8,128)S(1)}, f32[1,1]{1,0:T(1,128)}) custom-call(f32[256,1024]{1,0:T(8,128)S(1)} %copy-done, f32[1024,256]{1,0:T(8,128)S(1)} %copy-done.1), custom_call_target="tpu_custom_call" | custom-call | tf_op jit(solution)/shard_map/pallas_call | solution.py:275
  57.7 0.7 %copy.6 = f32[256,256]{1,0:T(8,128)} copy(f32[256,256]{1,0:T(8,128)S(1)} %get-tuple-element.8) | data formatting | bytes 524288
Async XLA Ops:
  0.6 1.2 %copy-start = (f32[256,1024]{1,0:T(8,128)S(1)}, f32[256,1024]{1,0:T(8,128)}, u32[]{:S(2)}) copy-start(f32[256,1024]{1,0:T(8,128)} %z_hbm.1) | copy-start | bytes 3145732
  1.9 1.2 %copy-start.1 = (f32[1024,256]{1,0:T(8,128)S(1)}, f32[1024,256]{1,0:T(8,128)}, u32[]{:S(2)}) copy-start(f32[1024,256]{1,0:T(8,128)} %s_hbm.1) | copy-start | bytes 3145732

commit v2 on v1

--- a/solution.py
+++ b/solution.py
@@ -13,11 +13,21 @@
 B = 16
 F32 = jnp.float32
 PARTS = 4
-CUT1, CUT2 = 9, 12
+VMEM_GRANT = 56_000_000
+CUT1, CUT2 = 7, 11
 
 
 def contract(a, b, da, db):
     return lax.dot_general(a, b, (((da,), (db,)), ((), ())), precision=HI, preferred_element_type=F32)
+
+
+def contract3(a, b, da, db):
+    def term(x, y):
+        return lax.dot_general(x, y, (((da,), (db,)), ((), ())), preferred_element_type=F32)
+
+    a1, b1 = a.astype(jnp.bfloat16), b.astype(jnp.bfloat16)
+    a2, b2 = (a - a1.astype(F32)).astype(jnp.bfloat16), (b - b1.astype(F32)).astype(jnp.bfloat16)
+    return term(a1, b1) + (term(a1, b2) + term(a2, b1))
 
 
 def split3(x):
@@ -166,13 +176,13 @@
     for i in range(PARTS):
         loads[2 * i].wait()
         loads[2 * i + 1].wait()
-        term = contract(z_ref[:, part(i)], s_ref[part(i), :], 1, 0)
+        term = contract3(z_ref[:, part(i)], s_ref[part(i), :], 1, 0)
         w_ref[...] = term if i == 0 else w_ref[...] + term
-    x_ref[half_rows(other), :] = contract(w_ref[:, half_rows(other)], z_ref[...], 0, 0)
+    x_ref[half_rows(other), :] = contract3(w_ref[:, half_rows(other)].T, z_ref[...], 1, 0)
     pl.semaphore_wait(barrier, len(greet))
     pair = remote(x_ref.at[half_rows(other), :], pair_ref, pair_s, pair_r, at(mq, other, mz))
     pair.start()
-    x_ref[half_rows(mc), :] = contract(w_ref[:, half_rows(mc)], z_ref[...], 0, 0)
+    x_ref[half_rows(mc), :] = contract3(w_ref[:, half_rows(mc)].T, z_ref[...], 1, 0)
     pair.wait()
     x_ref[half_rows(mc), :] = x_ref[half_rows(mc), :] + pair_ref[...]
 
@@ -223,14 +233,14 @@
             forward(i).start()
         if i > 0:
             forward(i - 1).wait_recv()
-            part_ref[...] = contract(m1_ref[...], full_ref[:, part(i - 1)], 1, 0)
+            part_ref[...] = contract3(m1_ref[...], full_ref[:, part(i - 1)], 1, 0)
             square = contract(part_ref[...], part_ref[...], 1, 1)
             m2_ref[...] = square if i == 1 else m2_ref[...] + square
-            term = contract(z_ref[:, part(i - 1)], part_ref[...], 1, 1)
+            term = contract3(z_ref[:, part(i - 1)], part_ref[...], 1, 1)
             w_ref[...] = term if i == 1 else w_ref[...] + term
 
     factor_steps(m2_ref, 0, steps)
-    compressed = contract(w_ref[...], m2_ref[...], 1, 1)
+    compressed = contract3(w_ref[...], m2_ref[...], 1, 1)
     c_ref[...] = compressed
     energy_kept = jnp.sum(compressed * compressed)
 
@@ -306,7 +316,7 @@
             dma((2 * nz - 1,)),
         ],
         compiler_params=pltpu.CompilerParams(
-            collective_id=0, has_side_effects=True, vmem_limit_bytes=40 * 2**20
+            collective_id=0, has_side_effects=True, vmem_limit_bytes=VMEM_GRANT
         ),
     )(factor, start_block)
     return compressed, tail[0, 0]

time: 60.4 us -> 56.7 us (0.939)
  local copies, waits for them, and re-layouts: 3.15 us -> 0.71 us
  Pallas kernels: 54.6 us -> 53.5 us
    unnamed x5 -> x1, local copies, waits for them, and re-layouts: 3.15 us -> 0.71 us
    pallas_call x1, Pallas kernels: 54.6 us -> 53.5 us  [local(): pl.pallas_call(functools.partial(kernel, sizes), out_shape=(jax.ShapeDtyp...]
where the time goes in v2:
time: 56.7 us; the launch traced here: 56.5 us
  Pallas kernels  53.5 us (94%)
  between operations  2.33 us (4%)
  local copies, waits for them, and re-layouts  0.71 us (1%)
    pallas_call x1, Pallas kernels, local(): pl.pallas_call(functools.partial(kernel, sizes), out_shape=(jax.ShapeDtyp...  53.5 us

profile of v2, /device:TPU:1, one launch (start us, length us, event | category | flops | bytes accessed | tf_op | source)
XLA Modules:
  0.0 56.5 jit_solution(12497063473726666609)
XLA Ops:
  0.6 53.5 %shard_map.41 = (f32[256,256]{1,0:T(8,128)S(1)}, f32[1,1]{1,0:T(1,128)}) custom-call(f32[256,1024]{1,0:T(8,128)} %z_hbm.1, f32[1024,256]{1,0:T(8,128)} %s_hbm.1), custom_call_target="tpu_custom_call" | custom-call | tf_op jit(solution)/shard_map/pallas_call | solution.py:285
  54.1 0.7 %copy.6 = f32[256,256]{1,0:T(8,128)} copy(f32[256,256]{1,0:T(8,128)S(1)} %get-tuple-element.8) | data formatting | bytes 524288

commit v3 on v2

--- a/solution.py
+++ b/solution.py
@@ -14,7 +14,8 @@
 F32 = jnp.float32
 PARTS = 4
 VMEM_GRANT = 56_000_000
-CUT1, CUT2 = 7, 11
+ORDER = (0, 2, 1, 3)
+CUTS = (0, 6, 8, 13, 16)
 
 
 def contract(a, b, da, db):
@@ -109,8 +110,11 @@
     w_ref,
     x_ref,
     pair_ref,
-    plane_ref,
+    near_ref,
+    mid_ref,
+    next_ref,
     line_ref,
+    most_ref,
     full_ref,
     part_ref,
     m1_ref,
@@ -121,7 +125,7 @@
     *sems,
 ):
     nx, ny, nz = sizes
-    (z_in, s_in, pair_s, pair_r, plane_s, plane_r, line_s, line_r, back_s, back_r, fw_s, fw_r, ep_s, ep_r, eq_s, eq_r) = sems
+    (z_in, s_in, pair_s, pair_r, near_s, near_r, next_s, next_r, line_s, line_r, back_s, back_r, fw_s, fw_r, ep_s, ep_r, eq_s, eq_r) = sems
     nq = nx * ny
     rank, depth = s_ref.shape[1], s_ref.shape[0]
     half = rank // 2
@@ -143,6 +147,7 @@
     plane.sort(key=lambda d: (-far(d[0], nx) - far(d[1], ny), d))
     line = sorted(range(1, nz), key=lambda d: (-far(d, nz), d))
     other = 1 - mc
+    distances = sorted(range(1, nx), key=lambda d: (-far(d, nx), d))
 
     def part(i):
         return pl.ds(i * cols, cols)
@@ -173,28 +178,35 @@
     def slab_rows(c, q):
         return pl.ds(pl.multiple_of(c * half + q * rows, rows), rows)
 
+    def image_rows(c):
+        return contract3(w_ref[:, half_rows(c)].T, z_ref[...], 1, 0).reshape(nx, ny, rows, depth)
+
     for i in range(PARTS):
         loads[2 * i].wait()
         loads[2 * i + 1].wait()
         term = contract3(z_ref[:, part(i)], s_ref[part(i), :], 1, 0)
         w_ref[...] = term if i == 0 else w_ref[...] + term
-    x_ref[half_rows(other), :] = contract3(w_ref[:, half_rows(other)].T, z_ref[...], 1, 0)
+    x_ref[other] = image_rows(other)
     pl.semaphore_wait(barrier, len(greet))
-    pair = remote(x_ref.at[half_rows(other), :], pair_ref, pair_s, pair_r, at(mq, other, mz))
+    pair = remote(x_ref.at[other], pair_ref, pair_s, pair_r, at(mq, other, mz))
     pair.start()
-    x_ref[half_rows(mc), :] = contract3(w_ref[:, half_rows(mc)].T, z_ref[...], 1, 0)
+    x_ref[mc] = image_rows(mc)
     pair.wait()
-    x_ref[half_rows(mc), :] = x_ref[half_rows(mc), :] + pair_ref[...]
-
-    for i in range(PARTS):
-        for j, (dx, dy) in enumerate(plane):
-            q = plane_peer(dx, dy)
-            remote(
-                x_ref.at[slab_rows(mc, q), part(i)], plane_ref.at[i, j], plane_s.at[i], plane_r.at[i], at(q, mc, mz)
-            ).start()
-
-    def plane_all(i, send, recv):
-        return remote(plane_ref.at[i], plane_ref.at[i], send.at[i], recv.at[i], at(mq, other, mz))
+    x_ref[mc] = x_ref[mc] + pair_ref[...]
+
+    def x_first(i):
+        return i < PARTS // 2
+
+    def terms(i, tx, ty):
+        return x_ref.at[mc, tx, :, :, part(i)] if x_first(i) else x_ref.at[mc, :, ty, :, part(i)]
+
+    for i in ORDER:
+        for j, d in enumerate(distances):
+            tx, ty = ((mx + d) % nx, my) if x_first(i) else (mx, (my + d) % ny)
+            remote(terms(i, tx, ty), near_ref.at[i, j], near_s.at[i], near_r.at[i], at(tx * ny + ty, mc, mz)).start()
+
+    def everything(ref, i, send, recv):
+        return remote(ref.at[i], ref.at[i], send.at[i], recv.at[i], at(mq, other, mz))
 
     def line_all(i):
         most = line_ref.at[i, pl.ds(0, nz - 1)]
@@ -202,42 +214,59 @@
 
     m1_ref[...] = contract(s_ref[...], s_ref[...], 0, 0)
     steps = rank // B
-    cut1, cut2 = steps * CUT1 // 16, steps * CUT2 // 16
-    factor_steps(m1_ref, 0, cut1)
-    for i in range(PARTS):
-        plane_all(i, plane_s, plane_r).wait_recv()
-        total = x_ref[slab_rows(mc, mq), part(i)]
-        for j in range(len(plane)):
-            total = total + plane_ref[i, j]
+    cuts = [steps * cut // 16 for cut in CUTS]
+    factor_steps(m1_ref, cuts[0], cuts[1])
+    for i in ORDER:
+        everything(near_ref, i, near_s, near_r).wait_recv()
+        total = terms(i, mx, my)[...]
+        for j in range(len(distances)):
+            total = total + near_ref[i, j]
+        mid_ref[i] = total
+        for j, d in enumerate(distances):
+            tx, ty = (mx, (my + d) % ny) if x_first(i) else ((mx + d) % nx, my)
+            block = mid_ref.at[i, ty if x_first(i) else tx]
+            remote(block, next_ref.at[i, j], next_s.at[i], next_r.at[i], at(tx * ny + ty, mc, mz)).start()
+    factor_steps(m1_ref, cuts[1], cuts[2])
+    for i in ORDER:
+        everything(next_ref, i, next_s, next_r).wait_recv()
+        total = mid_ref[i, my if x_first(i) else mx]
+        for j in range(len(distances)):
+            total = total + next_ref[i, j]
         line_ref[i, mz] = total
         own = line_ref.at[i, mz]
         for dz in line:
             remote(own, own, line_s.at[i], line_r.at[i], at(mq, mc, (mz + dz) % nz)).start()
-    factor_steps(m1_ref, cut1, cut2)
-    for i in range(PARTS):
+    factor_steps(m1_ref, cuts[2], cuts[3])
+    for i in ORDER:
         line_all(i).wait_recv()
         full_ref[slab_rows(mc, mq), part(i)] = functools.reduce(jnp.add, [line_ref[i, z] for z in range(nz)])
         slab = full_ref.at[slab_rows(mc, mq), part(i)]
         for dx, dy in plane:
             remote(slab, slab, back_s.at[i], back_r.at[i], at(plane_peer(dx, dy), mc, mz)).start()
-    factor_steps(m1_ref, cut2, steps)
+    factor_steps(m1_ref, cuts[3], cuts[4])
     energy_all = jnp.sum(z_ref[...] * z_ref[...])
 
     def forward(i):
         block = full_ref.at[half_rows(mc), part(i)]
         return remote(block, block, fw_s.at[i], fw_r.at[i], at(mq, other, mz))
 
-    for i in range(PARTS + 1):
-        if i < PARTS:
-            plane_all(i, back_s, back_r).wait_recv()
+    def gathered(i):
+        most = most_ref.at[pl.ds(0, nq - 1)]
+        return remote(most, most, back_s.at[i], back_r.at[i], at(mq, other, mz))
+
+    for place in range(PARTS + 1):
+        if place < PARTS:
+            i = ORDER[place]
+            gathered(i).wait_recv()
             forward(i).start()
-        if i > 0:
-            forward(i - 1).wait_recv()
-            part_ref[...] = contract3(m1_ref[...], full_ref[:, part(i - 1)], 1, 0)
+        if place > 0:
+            i = ORDER[place - 1]
+            forward(i).wait_recv()
+            part_ref[...] = contract3(m1_ref[...], full_ref[:, part(i)], 1, 0)
             square = contract(part_ref[...], part_ref[...], 1, 1)
-            m2_ref[...] = square if i == 1 else m2_ref[...] + square
-            term = contract3(z_ref[:, part(i - 1)], part_ref[...], 1, 1)
-            w_ref[...] = term if i == 1 else w_ref[...] + term
+            m2_ref[...] = square if place == 1 else m2_ref[...] + square
+            term = contract3(z_ref[:, part(i)], part_ref[...], 1, 1)
+            w_ref[...] = term if place == 1 else w_ref[...] + term
 
     factor_steps(m2_ref, 0, steps)
     compressed = contract3(w_ref[...], m2_ref[...], 1, 1)
@@ -263,9 +292,10 @@
         )
         second[-1].start()
     for i in range(PARTS):
-        plane_all(i, plane_s, plane_r).wait_send()
+        everything(near_ref, i, near_s, near_r).wait_send()
+        everything(next_ref, i, next_s, next_r).wait_send()
         line_all(i).wait_send()
-        plane_all(i, back_s, back_r).wait_send()
+        gathered(i).wait_send()
         forward(i).wait_send()
     for copy in second:
         copy.wait()
@@ -294,10 +324,13 @@
             pltpu.VMEM(factor.shape, F32),
             pltpu.VMEM(start_block.shape, F32),
             pltpu.VMEM((factor.shape[0], rank), F32),
-            pltpu.VMEM((rank, depth), F32),
-            pltpu.VMEM((half, depth), F32),
-            pltpu.VMEM((PARTS, nq - 1, rows, cols), F32),
+            pltpu.VMEM((2, nx, ny, rows, depth), F32),
+            pltpu.VMEM((nx, ny, rows, depth), F32),
+            pltpu.VMEM((PARTS, nx - 1, nx, rows, cols), F32),
+            pltpu.VMEM((PARTS, nx, rows, cols), F32),
+            pltpu.VMEM((PARTS, nx - 1, rows, cols), F32),
             pltpu.VMEM((PARTS, nz, rows, cols), F32),
+            pltpu.VMEM((nq, rows, cols), F32),
             pltpu.VMEM((rank, depth), F32),
             pltpu.VMEM((rank, cols), F32),
             pltpu.VMEM((rank, rank), F32),
@@ -309,7 +342,7 @@
             dma((PARTS,)),
             dma,
             dma,
-            *[dma((PARTS,)) for _ in range(8)],
+            *[dma((PARTS,)) for _ in range(10)],
             dma((nq - 1,)),
             dma((nq - 1,)),
             dma((2 * nz - 1,)),

time: 56.7 us -> 57.8 us (1.019)
  Pallas kernels: 53.5 us -> 54.6 us
    pallas_call x1, Pallas kernels: 53.5 us -> 54.6 us  [local(): pl.pallas_call(functools.partial(kernel, sizes), out_shape=(jax.ShapeDtyp...]
where the time goes in v3:
time: 57.8 us; the launch traced here: 57.7 us
  Pallas kernels  54.6 us (94%)
  between operations  2.33 us (4%)
  local copies, waits for them, and re-layouts  0.71 us (1%)
    pallas_call x1, Pallas kernels, local(): pl.pallas_call(functools.partial(kernel, sizes), out_shape=(jax.ShapeDtyp...  54.6 us

profile of v3, /device:TPU:1, one launch (start us, length us, event | category | flops | bytes accessed | tf_op | source)
XLA Modules:
  0.0 57.7 jit_solution(3293068294364750792)
XLA Ops:
  0.6 54.6 %shard_map.41 = (f32[256,256]{1,0:T(8,128)S(1)}, f32[1,1]{1,0:T(1,128)}) custom-call(f32[256,1024]{1,0:T(8,128)} %z_hbm.1, f32[1024,256]{1,0:T(8,128)} %s_hbm.1), custom_call_target="tpu_custom_call" | custom-call | tf_op jit(solution)/shard_map/pallas_call | solution.py:315
  55.3 0.7 %copy.6 = f32[256,256]{1,0:T(8,128)} copy(f32[256,256]{1,0:T(8,128)S(1)} %get-tuple-element.8) | data formatting | bytes 524288

commit v4 on v2

--- a/solution.py
+++ b/solution.py
@@ -11,23 +11,27 @@
 AXES = ("rows", "grp")
 HI = lax.Precision.HIGHEST
 B = 16
+PANEL1, PANEL2 = 32, 64
 F32 = jnp.float32
 PARTS = 4
 VMEM_GRANT = 56_000_000
-CUT1, CUT2 = 7, 11
+CUT1, CUT2 = 8, 12
 
 
 def contract(a, b, da, db):
     return lax.dot_general(a, b, (((da,), (db,)), ((), ())), precision=HI, preferred_element_type=F32)
 
 
-def contract3(a, b, da, db):
+def split2(x):
+    a = x.astype(jnp.bfloat16)
+    return a, (x - a.astype(F32)).astype(jnp.bfloat16)
+
+
+def product3(a, b, da, db):
     def term(x, y):
         return lax.dot_general(x, y, (((da,), (db,)), ((), ())), preferred_element_type=F32)
 
-    a1, b1 = a.astype(jnp.bfloat16), b.astype(jnp.bfloat16)
-    a2, b2 = (a - a1.astype(F32)).astype(jnp.bfloat16), (b - b1.astype(F32)).astype(jnp.bfloat16)
-    return term(a1, b1) + (term(a1, b2) + term(a2, b1))
+    return term(a[0], b[0]) + (term(a[0], b[1]) + term(a[1], b[0]))
 
 
 def split3(x):
@@ -37,65 +41,86 @@
     return a, b, (rest - b).astype(jnp.bfloat16).astype(F32)
 
 
-def factor_step(m_ref, k):
+def factor_step(m_ref, left_ref, right_ref, k):
     n = m_ref.shape[1]
-    per = 128 // B
-    row0 = pl.multiple_of(k * B, B)
-    half = pl.multiple_of((k // per) * 128, 128)
-    lane0 = (k % per) * B
+    panel_rows = right_ref.shape[0] // 6
+    row0 = pl.multiple_of(k * panel_rows, panel_rows)
+    groups = panel_rows // 8
     rows8 = lax.broadcasted_iota(jnp.int32, (8, 128), 0)
-    diag = [m_ref[pl.ds(row0 + 8 * g, 8), pl.ds(half, 128)] for g in range(2)]
-    column = {}
-    for c in range(B):
-        idx = jnp.full((8, 128), lane0 + c, jnp.int32)
-        for g in range(2):
-            if 8 * g + 8 > c:
-                column[c, g] = jnp.take_along_axis(diag[g], idx, axis=1)
-    lanes = lax.broadcasted_iota(jnp.int32, (8, n), 1) - k * B
-    in_block = (lanes >= 0) & (lanes < B)
-    wide = []
-    for g in range(2):
-        unit = jnp.where(lanes == 8 * g + lax.broadcasted_iota(jnp.int32, (8, n), 0), 1.0, 0.0)
-        wide.append(jnp.where(in_block, unit, m_ref[pl.ds(row0 + 8 * g, 8), :]))
-    pivots = [jnp.ones((8, 128), F32) for _ in range(2)]
-    for c in range(B):
-        gc, rc = divmod(c, 8)
-        pivot = jnp.broadcast_to(column[c, gc][rc : rc + 1, :], (8, 128))
-        pivots[gc] = jnp.where(rows8 == rc, pivot, pivots[gc])
-        scale = 1.0 / pivot
-        mult = {g: column[c, g] * scale for g in range(gc, 2)}
-        mult[gc] = jnp.where(rows8 > rc, mult[gc], 0.0)
-        pivot_row = jnp.broadcast_to(wide[gc][rc : rc + 1, :], (8, n))
-        for d in range(c + 1, B):
-            gd, rd = divmod(d, 8)
-            entry = jnp.broadcast_to(column[c, gd][rd : rd + 1, :], (8, 128))
-            for g in range(gd, 2):
-                column[d, g] = column[d, g] - mult[g] * entry
-        for g in range(gc, 2):
-            wide[g] = wide[g] - jnp.tile(mult[g], (1, n // 128)) * pivot_row
+    left, right = left_ref[...], right_ref[...]
+    own = jnp.dot(left_ref[pl.ds(row0, panel_rows), :], right, preferred_element_type=F32)
+    lanes = lax.broadcasted_iota(jnp.int32, (panel_rows, n), 1) - row0
+    panel = jnp.where((lanes >= -panel_rows) & (lanes < 0), 0.0, m_ref[pl.ds(row0, panel_rows), :]) - own
+    cols = lax.broadcasted_iota(jnp.int32, (n, n), 1) - row0
+    update = jnp.dot(left, right, preferred_element_type=F32)
+    below = lax.broadcasted_iota(jnp.int32, (n, n), 0) >= row0
+    m_ref[...] = jnp.where(below & (cols >= -panel_rows) & (cols < 0), 0.0, m_ref[...]) - update
+    wide = [panel[8 * g : 8 * g + 8] for g in range(groups)]
+    pivots = [jnp.ones((8, 128), F32) for _ in range(groups)]
+    lane8 = lanes[:8]
+    place8 = lax.broadcasted_iota(jnp.int32, (8, n), 0)
+    upper = row0 >= 128
+    for b in range(panel_rows // B):
+        first = b * B // 8
+        lane0 = row0 % 128 + b * B
+        column = {}
+        for c in range(B):
+            idx = jnp.full((8, 128), lane0 + c, jnp.int32)
+            for g in range(first + c // 8, groups):
+                column[c, g] = jnp.take_along_axis(jnp.where(upper, wide[g][:, 128:], wide[g][:, :128]), idx, axis=1)
+        in_block = (lane8 >= b * B) & (lane8 < b * B + B)
+        for g in range(first, groups):
+            unit = jnp.where(lane8 == 8 * g + place8, 1.0, 0.0) if g < first + B // 8 else 0.0
+            wide[g] = jnp.where(in_block, unit, wide[g])
+        for c in range(B):
+            gc, rc = first + c // 8, c % 8
+            pivot = jnp.broadcast_to(column[c, gc][rc : rc + 1, :], (8, 128))
+            pivots[gc] = jnp.where(rows8 == rc, pivot, pivots[gc])
+            scale = 1.0 / pivot
+            mult = {g: column[c, g] * scale for g in range(gc, groups)}
+            mult[gc] = jnp.where(rows8 > rc, mult[gc], 0.0)
+            pivot_row = jnp.broadcast_to(wide[gc][rc : rc + 1, :], (8, n))
+            for d in range(c + 1, B):
+                gd, rd = first + d // 8, d % 8
+                entry = jnp.broadcast_to(column[c, gd][rd : rd + 1, :], (8, 128))
+                for g in range(gd, groups):
+                    column[d, g] = column[d, g] - mult[g] * entry
+            for g in range(gc, groups):
+                wide[g] = wide[g] - jnp.tile(mult[g], (1, n // 128)) * pivot_row
     final = []
-    for g in range(2):
+    for g in range(groups):
         s = lax.rsqrt(pivots[g])
         s = s * (1.5 - 0.5 * pivots[g] * s * s)
         final.append(wide[g] * jnp.tile(s, (1, n // 128)))
     u = jnp.concatenate(final, axis=0)
+    inside = lax.broadcasted_iota(jnp.int32, (panel_rows, n), 0)
+    u = jnp.where((lanes < panel_rows) & (lanes > inside), 0.0, u)
     a, b, c = split3(u)
-    right = jnp.concatenate([a, b, a, c, b, a], axis=0).astype(jnp.bfloat16)
-    later = lax.broadcasted_iota(jnp.int32, (B, n), 1) >= (k + 1) * B
-    a, b, c = (jnp.where(later, t, 0.0) for t in (a, b, c))
-    left = jnp.concatenate([a, a, b, a, b, c], axis=0).T.astype(jnp.bfloat16)
-    update = jnp.dot(left, right, preferred_element_type=F32)
-    cols = lax.broadcasted_iota(jnp.int32, (n, n), 1) - k * B
-    m_ref[...] = jnp.where((cols >= 0) & (cols < B), 0.0, m_ref[...]) - update
-    m_ref[pl.ds(row0, B), :] = u
-
-
-def factor_steps(m_ref, lo, hi):
+    right_ref[...] = jnp.concatenate([a, b, a, c, b, a], axis=0).astype(jnp.bfloat16)
+    a, b, c = (jnp.where(lanes >= panel_rows, t, 0.0) for t in (a, b, c))
+    left_ref[...] = jnp.concatenate([a, a, b, a, b, c], axis=0).T.astype(jnp.bfloat16)
+    m_ref[pl.ds(row0, panel_rows), :] = u
+
+
+def factor_steps(refs, lo, hi):
+    m_ref, left_ref, right_ref = refs
+    n = m_ref.shape[1]
+    if lo == 0:
+        left_ref[...] = jnp.zeros_like(left_ref)
+        right_ref[...] = jnp.zeros_like(right_ref)
+
     def body(k, carry):
-        factor_step(m_ref, k)
+        factor_step(m_ref, left_ref, right_ref, k)
         return carry
 
     lax.fori_loop(lo, hi, body, 0)
+    if hi == steps_of(refs):
+        rows, cols = (lax.broadcasted_iota(jnp.int32, (n, n), d) for d in range(2))
+        m_ref[...] = jnp.where(rows >= cols, m_ref[...], 0.0)
+
+
+def steps_of(refs):
+    return refs[0].shape[0] * 6 // refs[2].shape[0]
 
 
 def kernel(
@@ -113,8 +138,14 @@
     line_ref,
     full_ref,
     part_ref,
+    z1_ref,
+    z2_ref,
     m1_ref,
+    left1_ref,
+    right1_ref,
     m2_ref,
+    left2_ref,
+    right2_ref,
     e_ref,
     ep_ref,
     eq_ref,
@@ -173,16 +204,28 @@
     def slab_rows(c, q):
         return pl.ds(pl.multiple_of(c * half + q * rows, rows), rows)
 
+    def halves(n):
+        return slice(0, n // 2), slice(n // 2, n)
+
+    def image_rows(c):
+        rows_of_c = split2(w_ref[:, half_rows(c)].T)
+        for h in halves(depth):
+            x_ref[half_rows(c), h] = product3(rows_of_c, (z1_ref[:, h], z2_ref[:, h]), 1, 0)
+
     for i in range(PARTS):
         loads[2 * i].wait()
         loads[2 * i + 1].wait()
-        term = contract3(z_ref[:, part(i)], s_ref[part(i), :], 1, 0)
-        w_ref[...] = term if i == 0 else w_ref[...] + term
-    x_ref[half_rows(other), :] = contract3(w_ref[:, half_rows(other)].T, z_ref[...], 1, 0)
+        parts = split2(z_ref[:, part(i)])
+        z1_ref[:, part(i)], z2_ref[:, part(i)] = parts
+        start = split2(s_ref[part(i), :])
+        for upper in halves(z_ref.shape[0]):
+            term = product3([p[upper] for p in parts], start, 1, 0)
+            w_ref[upper, :] = term if i == 0 else w_ref[upper, :] + term
+    image_rows(other)
     pl.semaphore_wait(barrier, len(greet))
     pair = remote(x_ref.at[half_rows(other), :], pair_ref, pair_s, pair_r, at(mq, other, mz))
     pair.start()
-    x_ref[half_rows(mc), :] = contract3(w_ref[:, half_rows(mc)].T, z_ref[...], 1, 0)
+    image_rows(mc)
     pair.wait()
     x_ref[half_rows(mc), :] = x_ref[half_rows(mc), :] + pair_ref[...]
 
@@ -201,9 +244,10 @@
         return remote(most, most, line_s.at[i], line_r.at[i], at(mq, other, mz))
 
     m1_ref[...] = contract(s_ref[...], s_ref[...], 0, 0)
-    steps = rank // B
+    start_factor = (m1_ref, left1_ref, right1_ref)
+    steps = steps_of(start_factor)
     cut1, cut2 = steps * CUT1 // 16, steps * CUT2 // 16
-    factor_steps(m1_ref, 0, cut1)
+    factor_steps(start_factor, 0, cut1)
     for i in range(PARTS):
         plane_all(i, plane_s, plane_r).wait_recv()
         total = x_ref[slab_rows(mc, mq), part(i)]
@@ -213,14 +257,15 @@
         own = line_ref.at[i, mz]
         for dz in line:
             remote(own, own, line_s.at[i], line_r.at[i], at(mq, mc, (mz + dz) % nz)).start()
-    factor_steps(m1_ref, cut1, cut2)
+    factor_steps(start_factor, cut1, cut2)
     for i in range(PARTS):
         line_all(i).wait_recv()
         full_ref[slab_rows(mc, mq), part(i)] = functools.reduce(jnp.add, [line_ref[i, z] for z in range(nz)])
         slab = full_ref.at[slab_rows(mc, mq), part(i)]
         for dx, dy in plane:
             remote(slab, slab, back_s.at[i], back_r.at[i], at(plane_peer(dx, dy), mc, mz)).start()
-    factor_steps(m1_ref, cut2, steps)
+    factor_steps(start_factor, cut2, steps)
+    start_inverse = split2(m1_ref[...])
     energy_all = jnp.sum(z_ref[...] * z_ref[...])
 
     def forward(i):
@@ -233,14 +278,15 @@
             forward(i).start()
         if i > 0:
             forward(i - 1).wait_recv()
-            part_ref[...] = contract3(m1_ref[...], full_ref[:, part(i - 1)], 1, 0)
+            part_ref[...] = product3(start_inverse, split2(full_ref[:, part(i - 1)]), 1, 0)
             square = contract(part_ref[...], part_ref[...], 1, 1)
             m2_ref[...] = square if i == 1 else m2_ref[...] + square
-            term = contract3(z_ref[:, part(i - 1)], part_ref[...], 1, 1)
+            term = product3((z1_ref[:, part(i - 1)], z2_ref[:, part(i - 1)]), split2(part_ref[...]), 1, 1)
             w_ref[...] = term if i == 1 else w_ref[...] + term
 
-    factor_steps(m2_ref, 0, steps)
-    compressed = contract3(w_ref[...], m2_ref[...], 1, 1)
+    image_factor = (m2_ref, left2_ref, right2_ref)
+    factor_steps(image_factor, 0, steps_of(image_factor))
+    compressed = product3(split2(w_ref[...]), split2(m2_ref[...]), 1, 1)
     c_ref[...] = compressed
     energy_kept = jnp.sum(compressed * compressed)
 
@@ -300,8 +346,14 @@
             pltpu.VMEM((PARTS, nz, rows, cols), F32),
             pltpu.VMEM((rank, depth), F32),
             pltpu.VMEM((rank, cols), F32),
+            pltpu.VMEM(factor.shape, jnp.bfloat16),
+            pltpu.VMEM(factor.shape, jnp.bfloat16),
             pltpu.VMEM((rank, rank), F32),
+            pltpu.VMEM((rank, 6 * PANEL1), jnp.bfloat16),
+            pltpu.VMEM((6 * PANEL1, rank), jnp.bfloat16),
             pltpu.VMEM((rank, rank), F32),
+            pltpu.VMEM((rank, 6 * PANEL2), jnp.bfloat16),
+            pltpu.VMEM((6 * PANEL2, rank), jnp.bfloat16),
             pltpu.VMEM((1, 128), F32),
             pltpu.VMEM((nq, 1, 128), F32),
             pltpu.VMEM((2 * nz, 1, 128), F32),

time: 56.7 us -> 54.5 us (0.961)
  Pallas kernels: 53.5 us -> 51.4 us
    pallas_call x1, Pallas kernels: 53.5 us -> 51.4 us  [local(): pl.pallas_call(functools.partial(kernel, sizes), out_shape=(jax.ShapeDtyp...]
where the time goes in v4:
time: 54.5 us; the launch traced here: 54.4 us
  Pallas kernels  51.4 us (94%)
  between operations  2.33 us (4%)
  local copies, waits for them, and re-layouts  0.71 us (1%)
    pallas_call x1, Pallas kernels, local(): pl.pallas_call(functools.partial(kernel, sizes), out_shape=(jax.ShapeDtyp...  51.4 us

profile of v4, /device:TPU:1, one launch (start us, length us, event | category | flops | bytes accessed | tf_op | source)
XLA Modules:
  0.0 54.4 jit_solution(4109590895673266126)
XLA Ops:
  0.6 51.4 %shard_map.41 = (f32[256,256]{1,0:T(8,128)S(1)}, f32[1,1]{1,0:T(1,128)}) custom-call(f32[256,1024]{1,0:T(8,128)} %z_hbm.1, f32[1024,256]{1,0:T(8,128)} %s_hbm.1), custom_call_target="tpu_custom_call" | custom-call | tf_op jit(solution)/shard_map/pallas_call | solution.py:331
  52.0 0.7 %copy.6 = f32[256,256]{1,0:T(8,128)} copy(f32[256,256]{1,0:T(8,128)S(1)} %get-tuple-element.8) | data formatting | bytes 524288

commit v5 on v4

--- a/solution.py
+++ b/solution.py
@@ -11,7 +11,7 @@
 AXES = ("rows", "grp")
 HI = lax.Precision.HIGHEST
 B = 16
-PANEL1, PANEL2 = 32, 64
+PANEL1, PANEL2 = 64, 64
 F32 = jnp.float32
 PARTS = 4
 VMEM_GRANT = 56_000_000
@@ -226,6 +226,8 @@
     pair = remote(x_ref.at[half_rows(other), :], pair_ref, pair_s, pair_r, at(mq, other, mz))
     pair.start()
     image_rows(mc)
+    for h in halves(rank):
+        m1_ref[h, :] = contract(s_ref[:, h], s_ref[...], 0, 0)
     pair.wait()
     x_ref[half_rows(mc), :] = x_ref[half_rows(mc), :] + pair_ref[...]
 
@@ -243,7 +245,6 @@
         most = line_ref.at[i, pl.ds(0, nz - 1)]
         return remote(most, most, line_s.at[i], line_r.at[i], at(mq, other, mz))
 
-    m1_ref[...] = contract(s_ref[...], s_ref[...], 0, 0)
     start_factor = (m1_ref, left1_ref, right1_ref)
     steps = steps_of(start_factor)
     cut1, cut2 = steps * CUT1 // 16, steps * CUT2 // 16

time: 54.5 us -> 54.4 us (level)
  no operation moved by 1% of the time
where the time goes in v5:
time: 54.4 us; the launch traced here: 54.2 us
  Pallas kernels  51.2 us (94%)
  between operations  2.33 us (4%)
  local copies, waits for them, and re-layouts  0.71 us (1%)
    pallas_call x1, Pallas kernels, local(): pl.pallas_call(functools.partial(kernel, sizes), out_shape=(jax.ShapeDtyp...  51.2 us

profile of v5, /device:TPU:1, one launch (start us, length us, event | category | flops | bytes accessed | tf_op | source)
XLA Modules:
  0.0 54.2 jit_solution(6697039087474426151)
XLA Ops:
  0.6 51.2 %shard_map.41 = (f32[256,256]{1,0:T(8,128)S(1)}, f32[1,1]{1,0:T(1,128)}) custom-call(f32[256,1024]{1,0:T(8,128)} %z_hbm.1, f32[1024,256]{1,0:T(8,128)} %s_hbm.1), custom_call_target="tpu_custom_call" | custom-call | tf_op jit(solution)/shard_map/pallas_call | solution.py:332
  51.8 0.7 %copy.6 = f32[256,256]{1,0:T(8,128)} copy(f32[256,256]{1,0:T(8,128)S(1)} %get-tuple-element.8) | data formatting | bytes 524288

commit v6 on v5

--- a/solution.py
+++ b/solution.py
@@ -13,7 +13,9 @@
 B = 16
 PANEL1, PANEL2 = 64, 64
 F32 = jnp.float32
-PARTS = 4
+LOADS = 4
+WIDTHS = (1, 2, 2, 2, 1)
+PARTS = len(WIDTHS)
 VMEM_GRANT = 56_000_000
 CUT1, CUT2 = 8, 12
 
@@ -156,7 +158,7 @@
     nq = nx * ny
     rank, depth = s_ref.shape[1], s_ref.shape[0]
     half = rank // 2
-    rows, cols = half // nq, depth // PARTS
+    rows, unit = half // nq, depth // sum(WIDTHS)
     me = lax.axis_index("rows")
     mz = lax.axis_index("grp")
     mc = me % 2
@@ -175,13 +177,19 @@
     line = sorted(range(1, nz), key=lambda d: (-far(d, nz), d))
     other = 1 - mc
 
+    def load_part(i):
+        return slice(i * (depth // LOADS), (i + 1) * (depth // LOADS))
+
     def part(i):
-        return pl.ds(i * cols, cols)
+        return slice(sum(WIDTHS[:i]) * unit, sum(WIDTHS[: i + 1]) * unit)
+
+    def width(i):
+        return slice(0, WIDTHS[i] * unit)
 
     loads = []
-    for i in range(PARTS):
-        loads.append(pltpu.make_async_copy(z_hbm.at[:, part(i)], z_ref.at[:, part(i)], z_in.at[i]))
-        loads.append(pltpu.make_async_copy(s_hbm.at[part(i), :], s_ref.at[part(i), :], s_in.at[i]))
+    for i in range(LOADS):
+        loads.append(pltpu.make_async_copy(z_hbm.at[:, load_part(i)], z_ref.at[:, load_part(i)], z_in.at[i]))
+        loads.append(pltpu.make_async_copy(s_hbm.at[load_part(i), :], s_ref.at[load_part(i), :], s_in.at[i]))
     for copy in loads:
         copy.start()
 
@@ -212,12 +220,12 @@
         for h in halves(depth):
             x_ref[half_rows(c), h] = product3(rows_of_c, (z1_ref[:, h], z2_ref[:, h]), 1, 0)
 
-    for i in range(PARTS):
+    for i in range(LOADS):
         loads[2 * i].wait()
         loads[2 * i + 1].wait()
-        parts = split2(z_ref[:, part(i)])
-        z1_ref[:, part(i)], z2_ref[:, part(i)] = parts
-        start = split2(s_ref[part(i), :])
+        parts = split2(z_ref[:, load_part(i)])
+        z1_ref[:, load_part(i)], z2_ref[:, load_part(i)] = parts
+        start = split2(s_ref[load_part(i), :])
         for upper in halves(z_ref.shape[0]):
             term = product3([p[upper] for p in parts], start, 1, 0)
             w_ref[upper, :] = term if i == 0 else w_ref[upper, :] + term
@@ -235,14 +243,15 @@
         for j, (dx, dy) in enumerate(plane):
             q = plane_peer(dx, dy)
             remote(
-                x_ref.at[slab_rows(mc, q), part(i)], plane_ref.at[i, j], plane_s.at[i], plane_r.at[i], at(q, mc, mz)
+                x_ref.at[slab_rows(mc, q), part(i)], plane_ref.at[i, j, :, width(i)], plane_s.at[i], plane_r.at[i], at(q, mc, mz)
             ).start()
 
     def plane_all(i, send, recv):
-        return remote(plane_ref.at[i], plane_ref.at[i], send.at[i], recv.at[i], at(mq, other, mz))
+        every = plane_ref.at[i, :, :, width(i)]
+        return remote(every, every, send.at[i], recv.at[i], at(mq, other, mz))
 
     def line_all(i):
-        most = line_ref.at[i, pl.ds(0, nz - 1)]
+        most = line_ref.at[i, pl.ds(0, nz - 1), :, width(i)]
         return remote(most, most, line_s.at[i], line_r.at[i], at(mq, other, mz))
 
     start_factor = (m1_ref, left1_ref, right1_ref)
@@ -253,15 +262,15 @@
         plane_all(i, plane_s, plane_r).wait_recv()
         total = x_ref[slab_rows(mc, mq), part(i)]
         for j in range(len(plane)):
-            total = total + plane_ref[i, j]
-        line_ref[i, mz] = total
-        own = line_ref.at[i, mz]
+            total = total + plane_ref[i, j, :, width(i)]
+        line_ref[i, mz, :, width(i)] = total
+        own = line_ref.at[i, mz, :, width(i)]
         for dz in line:
             remote(own, own, line_s.at[i], line_r.at[i], at(mq, mc, (mz + dz) % nz)).start()
     factor_steps(start_factor, cut1, cut2)
     for i in range(PARTS):
         line_all(i).wait_recv()
-        full_ref[slab_rows(mc, mq), part(i)] = functools.reduce(jnp.add, [line_ref[i, z] for z in range(nz)])
+        full_ref[slab_rows(mc, mq), part(i)] = functools.reduce(jnp.add, [line_ref[i, z, :, width(i)] for z in range(nz)])
         slab = full_ref.at[slab_rows(mc, mq), part(i)]
         for dx, dy in plane:
             remote(slab, slab, back_s.at[i], back_r.at[i], at(plane_peer(dx, dy), mc, mz)).start()
@@ -279,10 +288,11 @@
             forward(i).start()
         if i > 0:
             forward(i - 1).wait_recv()
-            part_ref[...] = product3(start_inverse, split2(full_ref[:, part(i - 1)]), 1, 0)
-            square = contract(part_ref[...], part_ref[...], 1, 1)
+            image = part_ref.at[:, width(i - 1)]
+            image[...] = product3(start_inverse, split2(full_ref[:, part(i - 1)]), 1, 0)
+            square = contract(image[...], image[...], 1, 1)
             m2_ref[...] = square if i == 1 else m2_ref[...] + square
-            term = product3((z1_ref[:, part(i - 1)], z2_ref[:, part(i - 1)]), split2(part_ref[...]), 1, 1)
+            term = product3((z1_ref[:, part(i - 1)], z2_ref[:, part(i - 1)]), split2(image[...]), 1, 1)
             w_ref[...] = term if i == 1 else w_ref[...] + term
 
     image_factor = (m2_ref, left2_ref, right2_ref)
@@ -325,7 +335,7 @@
     nq = nx * ny
     depth, rank = start_block.shape
     half = rank // 2
-    rows, cols = half // nq, depth // PARTS
+    rows, cols = half // nq, depth // sum(WIDTHS) * max(WIDTHS)
     vmem = pl.BlockSpec(memory_space=pltpu.VMEM)
     hbm = pl.BlockSpec(memory_space=pltpu.HBM)
     dma = pltpu.SemaphoreType.DMA
@@ -358,8 +368,8 @@
             pltpu.VMEM((1, 128), F32),
             pltpu.VMEM((nq, 1, 128), F32),
             pltpu.VMEM((2 * nz, 1, 128), F32),
-            dma((PARTS,)),
-            dma((PARTS,)),
+            dma((LOADS,)),
+            dma((LOADS,)),
             dma,
             dma,
             *[dma((PARTS,)) for _ in range(8)],

time: 54.4 us -> 55.1 us (1.013)
  Pallas kernels: 51.2 us -> 51.9 us
    pallas_call x1, Pallas kernels: 51.2 us -> 51.9 us  [local(): pl.pallas_call(functools.partial(kernel, sizes), out_shape=(jax.ShapeDtyp...]
where the time goes in v6:
time: 55.1 us; the launch traced here: 55 us
  Pallas kernels  51.9 us (94%)
  between operations  2.33 us (4%)
  local copies, waits for them, and re-layouts  0.71 us (1%)
    pallas_call x1, Pallas kernels, local(): pl.pallas_call(functools.partial(kernel, sizes), out_shape=(jax.ShapeDtyp...  51.9 us

profile of v6, /device:TPU:1, one launch (start us, length us, event | category | flops | bytes accessed | tf_op | source)
XLA Modules:
  0.0 55.0 jit_solution(12342773765667143255)
XLA Ops:
  0.6 51.9 %shard_map.41 = (f32[256,256]{1,0:T(8,128)S(1)}, f32[1,1]{1,0:T(1,128)}) custom-call(f32[256,1024]{1,0:T(8,128)} %z_hbm.1, f32[1024,256]{1,0:T(8,128)} %s_hbm.1), custom_call_target="tpu_custom_call" | custom-call | tf_op jit(solution)/shard_map/pallas_call | solution.py:342
  52.6 0.7 %copy.6 = f32[256,256]{1,0:T(8,128)} copy(f32[256,256]{1,0:T(8,128)S(1)} %get-tuple-element.8) | data formatting | bytes 524288

commit v7 on v6

--- a/solution.py
+++ b/solution.py
@@ -14,7 +14,7 @@
 PANEL1, PANEL2 = 64, 64
 F32 = jnp.float32
 LOADS = 4
-WIDTHS = (1, 2, 2, 2, 1)
+WIDTHS = (3, 3, 2)
 PARTS = len(WIDTHS)
 VMEM_GRANT = 56_000_000
 CUT1, CUT2 = 8, 12

time: 55.1 us -> 55.8 us (1.013)
  Pallas kernels: 51.9 us -> 52.6 us
    pallas_call x1, Pallas kernels: 51.9 us -> 52.6 us  [local(): pl.pallas_call(functools.partial(kernel, sizes), out_shape=(jax.ShapeDtyp...]
where the time goes in v7:
time: 55.8 us; the launch traced here: 55.7 us
  Pallas kernels  52.6 us (94%)
  between operations  2.33 us (4%)
  local copies, waits for them, and re-layouts  0.71 us (1%)
    pallas_call x1, Pallas kernels, local(): pl.pallas_call(functools.partial(kernel, sizes), out_shape=(jax.ShapeDtyp...  52.6 us

profile of v7, /device:TPU:1, one launch (start us, length us, event | category | flops | bytes accessed | tf_op | source)
XLA Modules:
  0.0 55.7 jit_solution(6390109044112656989)
XLA Ops:
  0.6 52.6 %shard_map.41 = (f32[256,256]{1,0:T(8,128)S(1)}, f32[1,1]{1,0:T(1,128)}) custom-call(f32[256,1024]{1,0:T(8,128)} %z_hbm.1, f32[1024,256]{1,0:T(8,128)} %s_hbm.1), custom_call_target="tpu_custom_call" | custom-call | tf_op jit(solution)/shard_map/pallas_call | solution.py:342
  53.3 0.7 %copy.6 = f32[256,256]{1,0:T(8,128)} copy(f32[256,256]{1,0:T(8,128)S(1)} %get-tuple-element.8) | data formatting | bytes 524288
